TPU v7x, 256 devices: a whole 4x4x8 slice. The times are simulated.
256 devices in a mesh: row: 8 (over y, z_lo), col: 8 (over z_hi, core), layer: 4 (over x).
Axes of the slice: x: 4, y: 4, z: 8 (z_hi: 4, z_lo: 2; z = z_hi * 2 + z_lo), core: 2. Of those that a mesh axis runs over, the one named last changes fastest.
Arguments:
- density_tiles: bfloat16 [192, 8, 2, 128, 128], P(('row', 'col')), may hold values from -1.5 to 1.5
- tile_columns: int32 [192, 8, 2], P(('row', 'col')), may hold values from -1 to 191, as said below
Outputs:
- square_tiles: bfloat16 [192, 8, 2, 128, 128], P(('row', 'col'), None, None, 'layer')
Inputs may be any that keep to these rules, and one draw needn't show every extreme that they name: `tile_columns`: entry [i, g, s] is a tile column in group g (columns g * 24 to (g + 1) * 24 - 1) or -1; within one block row and group the listed columns are distinct and empty slots come after the listed ones; block row i lists its own column i in the first slot of its group, whose 2 slots are all listed; other groups hold 0 to 2 listed tiles.
All inputs are finite; a program needn't handle non-finite values.
Results may differ from a plain program's by a relative error of at most 0.0048.
Values may be sent and summed in bfloat16 or wider, within the bound.
No kernel may reach another device: no remote copies, remote signals or barrier semaphores. Data moves between devices by JAX's collectives and lax.ppermute only.
A program may use at most 64 MiB of HBM per device.

v0:
```python
import jax
import jax.numpy as jnp
from jax import lax
from jax.sharding import Mesh
from jax.sharding import PartitionSpec as P

ROW = ("row_0", "row_1")
ROW_COL = ("row_0", "row_1", "col")


def filled_up(lines, devices):
    spare = -len(lines) % devices
    return jnp.pad(lines, [(0, spare)] + [(0, 0)] * (lines.ndim - 1))


def spread(array, axis, root):
    lines = jnp.where(lax.axis_index(axis) == root, array, jnp.zeros_like(array)).reshape(
        -1, *array.shape[1:][-1:]
    )
    padded = filled_up(lines, lax.axis_size(axis))
    own = lax.psum_scatter(padded, axis, scatter_dimension=0, tiled=True)
    return lax.all_gather(own, axis, axis=0, tiled=True)[: len(lines)].reshape(array.shape)


def broadcast_by_axis(array, axes, root):
    array = jnp.where(lax.axis_index(axes) == root, array, jnp.zeros_like(array))
    for axis in axes:
        array = lax.psum(array, axis)
    return array


def in_blocks(array, dim, devices):
    before, after = (array.shape[:dim], array.shape[dim + 1 :])
    return jnp.moveaxis(array.reshape(*before, devices, -1, *after), dim, 0)


def sent_and_summed(array, axis, dim):
    pieces = in_blocks(array, dim, lax.axis_size(axis))
    arrived = lax.all_to_all(pieces, axis, split_axis=0, concat_axis=0, tiled=True)
    return arrived.astype(jnp.float32).sum(axis=0)


def multiply(left_tiles, left_columns, right_tiles, right_columns, target_columns, start_row):
    is_live = left_columns >= 0
    inner_rows = jnp.where(is_live, left_columns - start_row, 0).astype(jnp.int32)
    inner_columns = right_columns[inner_rows]
    matches = (
        (inner_columns[:, :, None, :] == target_columns[:, None, :, None])
        & is_live[:, :, None, None]
        & (target_columns >= 0)[:, None, :, None]
    )
    slot_index = jnp.argmax(matches.astype(jnp.int32), axis=-1)
    located = jnp.any(matches, axis=-1)
    selected = right_tiles[inner_rows[:, :, None], slot_index]
    selected = jnp.where(located[:, :, :, None, None], selected, jnp.zeros((), jnp.bfloat16))
    return jnp.einsum("iarc,iascd->isrd", left_tiles, selected, preferred_element_type=jnp.float32)


def on_device(density_tiles, tile_columns):
    row_count = lax.axis_size(ROW)
    column_count = lax.axis_size("col")
    layer_count = lax.axis_size("layer")
    grid_tiles, grid_columns = (
        lax.all_to_all(density_tiles, "col", split_axis=1, concat_axis=0, tiled=True),
        lax.all_to_all(tile_columns, "col", split_axis=1, concat_axis=0, tiled=True),
    )
    block_tiles = grid_tiles[:, 0]
    block_columns = grid_columns[:, 0]
    group_rows = block_tiles.shape[0]
    row_ratio = column_count // row_count
    panel_rows = group_rows // row_ratio
    per_layer = column_count // layer_count
    layer_index = lax.axis_index("layer")
    partial_value = jnp.zeros(block_tiles.shape, jnp.float32)
    for panel_step in range(per_layer):
        panel_index = layer_index * per_layer + panel_step
        left_tiles, left_columns = (
            spread(block_tiles, "col", panel_index),
            spread(block_columns, "col", panel_index),
        )
        right_tiles, right_columns = (
            broadcast_by_axis(block_tiles, ROW, panel_index // row_ratio),
            broadcast_by_axis(block_columns, ROW, panel_index // row_ratio),
        )
        partial_value = partial_value + multiply(
            left_tiles,
            left_columns,
            right_tiles,
            right_columns,
            block_columns,
            panel_index * panel_rows,
        )
    rounded = partial_value.astype(jnp.bfloat16)
    summed = sent_and_summed(rounded.astype(jnp.float32).astype(jnp.bfloat16), "layer", 2)
    returned = lax.all_to_all(
        summed.astype(jnp.bfloat16)[:, None], "col", split_axis=0, concat_axis=1, tiled=True
    )
    return returned


def solution(mesh):
    split = Mesh(
        mesh.devices.reshape(4, 2, mesh.shape["col"], mesh.shape["layer"]),
        ("row_0", "row_1", "col", "layer"),
    )
    return jax.shard_map(
        on_device,
        mesh=split,
        in_specs=(P(ROW_COL, None, None, None, None), P(ROW_COL, None, None)),
        out_specs=P(ROW_COL, None, None, "layer", None),
        check_vma=False,
    )
```

profile of v0, /device:TPU:1, one launch (start us, length us, event | category | flops | bytes accessed | tf_op | source)
XLA Modules:
  0.0 319.0 jit_solution(11141987187466286460)
XLA Ops:
  7.4 2.7 copy.204
  10.1 10.0 %all-to-all-start.1 = ((bf16[3,8,2,128,128]{4,3,2,0,1:T(8,128)(2,1)}), bf16[3,8,2,128,128]{4,3,2,0,1:T(8,128)(2,1)S(1)}, u32[]{:S(2)}, u32[]{:S(2)}) async-start(bf16[3,8,2,128,128]{4,3,2,0,1:T(8,128)(2,1)} %copy.204), calls=%async_computation.1 | async-start | bytes 3145728 | tf_op jit(solution)/shard_map/all_to_all | solution.py:64
  20.1 33.3 %all-to-all-done.1 = bf16[3,8,2,128,128]{4,3,2,0,1:T(8,128)(2,1)S(1)} async-done(((bf16[3,8,2,128,128]{4,3,2,0,1:T(8,128)(2,1)}), bf16[3,8,2,128,128]{4,3,2,0,1:T(8,128)(2,1)S(1)}, u32[]{:S(2)}, u32[]{:S(2)}) %all-to-all-start.1) | async-done | bytes 1572896 | tf_op jit(solution)/shard_map/all_to_all | solution.py:64
  53.4 2.8 broadcast_select_fusion.2
  57.4 82.9 %all-reduce.10.cloned.1.call-done = (bf16[24,2,128,128]{3,2,1,0:T(8,128)(2,1)}, bf16[24,2,128,128]{3,2,1,0:T(8,128)(2,1)}) async-done(((bf16[24,2,128,128]{3,2,1,0:T(8,128)(2,1)}, bf16[24,2,128,128]{3,2,1,0:T(8,128)(2,1)}), (bf16[24,2,128,128]{3,2,1,0:T(8,128)(2,1)}, bf16[24,2,128,128]{3,2,1,0:T(8,128)(2,1)})) %all-reduce.10.cloned.1.call-update) | async-done | bytes 3145744 | tf_op jit(solution)/shard_map/psum | solution.py:28
  141.0 0.7 copy.187
  141.7 7.8 %all-to-all-start = ((s32[3,8,2]{0,2,1:T(2,128)}), s32[3,8,2]{0,2,1:T(2,128)S(1)}, u32[]{:S(2)}, u32[]{:S(2)}) async-start(s32[3,8,2]{0,2,1:T(2,128)} %copy.187), calls=%async_computation | async-start | bytes 16384 | tf_op jit(solution)/shard_map/all_to_all | solution.py:65
  150.7 5.9 %all-to-all-done = s32[3,8,2]{0,2,1:T(2,128)S(1)} async-done(((s32[3,8,2]{0,2,1:T(2,128)}), s32[3,8,2]{0,2,1:T(2,128)S(1)}, u32[]{:S(2)}, u32[]{:S(2)}) %all-to-all-start) | async-done | bytes 224 | tf_op jit(solution)/shard_map/all_to_all | solution.py:65
  156.8 25.1 %all-reduce.2 = (s32[24,2]{1,0:T(8,128)S(1)}, s32[24,2]{1,0:T(8,128)S(1)}) all-reduce(s32[24,2]{1,0:T(8,128)S(1)} %get-tuple-element.32, s32[24,2]{1,0:T(8,128)S(1)} %get-tuple-element.34), channel_id=4, replica_groups=mesh['row_0'=4,'row_1'=2,'col'=8,'layer'=4] {'col'}, use_global_device_ids=true, to_apply=%region_10.11.clone | all-reduce | flops 96 | bytes 768
  182.0 12.9 %all-gather = s32[8,3,2]{1,2,0:T(2,128)S(1)} all-gather(s32[1,3,2]{1,2,0:T(2,128)S(1)} %bitcast.110), channel_id=1, replica_groups=mesh['row_0'=4,'row_1'=2,'col'=8,'layer'=4] {'col'}, dimensions={0}, use_global_device_ids=true | all-gather | bytes 216 | tf_op jit(solution)/shard_map/all_gather | solution.py:22
  195.7 13.0 %all-gather.1 = s32[8,3,2]{1,2,0:T(2,128)S(1)} all-gather(s32[1,3,2]{1,2,0:T(2,128)S(1)} %bitcast.109), channel_id=1, replica_groups=mesh['row_0'=4,'row_1'=2,'col'=8,'layer'=4] {'col'}, dimensions={0}, use_global_device_ids=true | all-gather | bytes 216 | tf_op jit(solution)/shard_map/all_gather | solution.py:22
  209.6 13.5 %all-reduce.3 = (s32[24,2]{1,0:T(8,128)S(1)}, s32[24,2]{1,0:T(8,128)S(1)}) all-reduce(s32[24,2]{1,0:T(8,128)S(1)} %get-tuple-element.33, s32[24,2]{1,0:T(8,128)S(1)} %get-tuple-element.31), channel_id=1, replica_groups=mesh['row_0'=4,'row_1'=2,'col'=8,'layer'=4] {'row_0'}, use_global_device_ids=true, to_apply=%region_8.9 | all-reduce | flops 96 | bytes 768 | tf_op jit(solution)/shard_map/psum | solution.py:28
  223.0 7.7 %all-reduce.4 = (s32[24,2]{1,0:T(8,128)S(1)}, s32[24,2]{1,0:T(8,128)S(1)}) all-reduce(s32[24,2]{1,0:T(8,128)S(1)} %get-tuple-element.11, s32[24,2]{1,0:T(8,128)S(1)} %get-tuple-element.12), channel_id=1, replica_groups=mesh['row_0'=4,'row_1'=2,'col'=8,'layer'=4] {'row_1'}, use_global_device_ids=true, to_apply=%region_9.10 | all-reduce | flops 96 | bytes 768 | tf_op jit(solution)/shard_map/psum | solution.py:28
  232.7 0.6 iota_reduce_fusion
  233.5 0.6 iota_reduce_fusion.1
  234.4 11.8 %all-reduce.12.cloned.1.call-done = (bf16[24,2,128,128]{3,2,1,0:T(8,128)(2,1)}, bf16[24,2,128,128]{3,2,1,0:T(8,128)(2,1)}) async-done(((bf16[24,2,128,128]{3,2,1,0:T(8,128)(2,1)}, bf16[24,2,128,128]{3,2,1,0:T(8,128)(2,1)}), (bf16[24,2,128,128]{3,2,1,0:T(8,128)(2,1)}, bf16[24,2,128,128]{3,2,1,0:T(8,128)(2,1)})) %all-reduce.12.cloned.1.call-update) | async-done | bytes 3145744 | tf_op jit(solution)/shard_map/psum | solution.py:28
  246.2 4.5 %gather_fusion.3 = bf16[96,128,128]{2,1,0:T(8,128)(2,1)} fusion(bf16[24,2,128,128]{3,2,1,0:T(8,128)(2,1)} %get-tuple-element.17, s32[96]{0:T(128)S(1)} %reshape.87), kind=kCustom, calls=%fused_computation.3 | custom fusion | bytes 6292224 | tf_op jit(solution)/shard_map/gather | solution.py:54
  250.6 3.0 gather_fusion.1
  253.7 4.8 %fusion.1 = f32[24,2,128,128,1]{2,3,1,4,0:T(8,128)} fusion(bf16[24,2,128,128,1]{3,2,4,1,0:T(8,128)(2,1)} %bitcast.105, bf16[24,2,2,128,128]{4,3,2,1,0:T(8,128)(2,1)} %bitcast.95, pred[24,2,2]{2,1,0:T(4,128)(4,1)S(1)} %copy.219), kind=kOutput, calls=%fused_computation.6 | convolution fusion | flops 404226048 | bytes 7864416 | tf_op jit(solution)/shard_map/iarc,iascd->isrd/dot_general | solution.py:56
  258.5 5.5 %all-gather.5.cloned.1.call-done = bf16[6144,128]{1,0:T(8,128)(2,1)} async-done(((bf16[768,128]{1,0:T(8,128)(2,1)}), bf16[6144,128]{1,0:T(8,128)(2,1)}) %all-gather.5.cloned.1.call-update) | async-done | bytes 1572880 | tf_op jit(solution)/shard_map/all_gather | solution.py:22
  263.9 3.0 fusion
  267.4 24.0 %all_to_all.47 = bf16[4,24,2,32,128]{4,3,2,1,0:T(8,128)(2,1)S(1)} all-to-all(bf16[4,24,2,32,128]{4,3,2,1,0:T(8,128)(2,1)S(1)} %bitcast.97), channel_id=1, replica_groups=mesh['row_0'=4,'row_1'=2,'col'=8,'layer'=4] {'layer'}, dimensions={0} | all-to-all | bytes 3145728 | tf_op jit(solution)/shard_map/all_to_all | solution.py:39
  291.8 18.9 %all_to_all.48 = bf16[24,1,2,32,128]{4,3,2,1,0:T(8,128)(2,1)S(1)} all-to-all(bf16[24,1,2,32,128]{4,3,2,1,0:T(8,128)(2,1)S(1)} %bitcast.104), channel_id=1, replica_groups=mesh['row_0'=4,'row_1'=2,'col'=8,'layer'=4] {'col'}, dimensions={0} | all-to-all | bytes 786432 | tf_op jit(solution)/shard_map/all_to_all | solution.py:95
  310.6 0.8 copy.224
  (70 shorter events, 7.5 us)
Async XLA Ops:
  10.1 43.3 %all-to-all-start.1 = ((bf16[3,8,2,128,128]{4,3,2,0,1:T(8,128)(2,1)}), bf16[3,8,2,128,128]{4,3,2,0,1:T(8,128)(2,1)S(1)}, u32[]{:S(2)}, u32[]{:S(2)}) async-start(bf16[3,8,2,128,128]{4,3,2,0,1:T(8,128)(2,1)} %copy.204), calls=%async_computation.1 | async-start | bytes 3145728 | tf_op jit(solution)/shard_map/all_to_all | solution.py:64
  20.1 120.3 %all-reduce.10.cloned.1.call-start = ((), (), s32[]{:S(2)}) async-start(), calls=%async_computation.10 | async-start | bytes 6291456 | tf_op jit(solution)/shard_map/psum | solution.py:28
  56.2 84.2 %reduce-scatter.5.cloned.1.call-start = ((), (), s32[]{:S(2)}) async-start(), calls=%async_computation.8 | async-start | bytes 1769472 | tf_op jit(solution)/shard_map/reduce_scatter | solution.py:21
  56.8 138.2 %reduce-scatter.3.cloned.1.call-start = ((), (), s32[]{:S(2)}) async-start(), calls=%async_computation.6 | async-start | bytes 1769472 | tf_op jit(solution)/shard_map/reduce_scatter | solution.py:21
  57.4 188.8 %all-reduce.12.cloned.1.call-start = ((), (), s32[]{:S(2)}) async-start(), calls=%async_computation.11 | async-start | bytes 6291456 | tf_op jit(solution)/shard_map/psum | solution.py:28
  140.3 0.7 copy-start
  140.3 9.2 %copy-start.1 = (u32[256]{0:T(256)S(1)}, u32[256]{0:T(256)}, u32[]{:S(2)}) copy-start(u32[256]{0:T(256)} %constant.100) | copy-start | bytes 3076
  140.3 113.3 %all-gather.7.cloned.1.call-start = ((), (), s32[]{:S(2)}) async-start(), calls=%async_computation.9 | async-start | bytes 1769472 | tf_op jit(solution)/shard_map/all_gather | solution.py:22
  141.7 14.9 %all-to-all-start = ((s32[3,8,2]{0,2,1:T(2,128)}), s32[3,8,2]{0,2,1:T(2,128)S(1)}, u32[]{:S(2)}, u32[]{:S(2)}) async-start(s32[3,8,2]{0,2,1:T(2,128)} %copy.187), calls=%async_computation | async-start | bytes 16384 | tf_op jit(solution)/shard_map/all_to_all | solution.py:65
  149.5 114.4 %all-gather.5.cloned.1.call-start = ((), (), s32[]{:S(2)}) async-start(), calls=%async_computation.7 | async-start | bytes 1769472 | tf_op jit(solution)/shard_map/all_gather | solution.py:22
Sparse Core Ops, SparseCore 0:
  56.3 83.9 all-reduce.9
  143.0 103.1 all-reduce.11
Sparse Core Ops, SparseCore 1:
  59.3 43.9 reduce-scatter.4
  105.7 40.1 reduce-scatter.2
  147.6 63.6 all-gather.6
  213.1 50.8 all-gather.4
where the time goes:
time: 319 us
  waiting for transfers between devices  141 us (44%)
  blocking collectives  115 us (36%)
  starting transfers between devices  18 us (6%)
  local copies, waits for them, and re-layouts  16.9 us (5%)
  between operations  15.8 us (5%)
  matrix products  7.82 us (2%)
  other arithmetic  4.51 us (1%)
    psum x2, waiting for transfers between devices, broadcast_by_axis(): array = lax.psum(array, axis)  94.7 us
    all_to_all x1, waiting for transfers between devices, on_device(): lax.all_to_all(density_tiles, 'col', split_axis=1, concat_axis=0, tiled=T...  33.3 us
    all_gather x2, blocking collectives, spread(): lax.all_gather(own, axis, axis=0, tiled=True)[:len(lines)]  25.9 us
    unnamed x1, blocking collectives  25.1 us
    all_to_all x1, blocking collectives, sent_and_summed(): lax.all_to_all(pieces, axis, split_axis=0, concat_axis=0, tiled=True)  24 us
    psum x2, blocking collectives, broadcast_by_axis(): array = lax.psum(array, axis)  21.2 us
    all_to_all x1, blocking collectives, on_device(): lax.all_to_all(summed.astype(jnp.bfloat16)[:, None], 'col', split_axis=0,...  18.9 us
    all_to_all x1, starting transfers between devices, on_device(): lax.all_to_all(density_tiles, 'col', split_axis=1, concat_axis=0, tiled=T...  9.95 us
  transfers between devices with their start and end apart: 8, of which 5 were waited for; matrix products, arithmetic and copies ran while one was open for 6% of the time, Pallas kernels for 0%

commit v1 on v0

--- a/solution.py
+++ b/solution.py
@@ -19,7 +19,9 @@
     )
     padded = filled_up(lines, lax.axis_size(axis))
     own = lax.psum_scatter(padded, axis, scatter_dimension=0, tiled=True)
-    return lax.all_gather(own, axis, axis=0, tiled=True)[: len(lines)].reshape(array.shape)
+    return jnp.concatenate(
+        lax.all_to_all(jnp.stack([own] * lax.axis_size(axis)), axis, 0, 0), axis=0
+    )[: len(lines)].reshape(array.shape)
 
 
 def broadcast_by_axis(array, axes, root):

time: 319 us -> 351 us (1.10)
  starting transfers between devices: 18 us -> 41.7 us
  local copies, waits for them, and re-layouts: 16.9 us -> 22.1 us
    all_gather x2 -> x0, blocking collectives: 25.9 us -> none  [spread(): lax.all_gather(own, axis, axis=0, tiled=True)[:len(lines)]]
    all_to_all x0 -> x3, starting transfers between devices: none -> 21.5 us  [spread(): lax.all_to_all(jnp.stack([own] * lax.axis_size(axis)), axis, 0, 0)]
    psum x2, blocking collectives: 21.2 us -> 39.1 us  [broadcast_by_axis(): array = lax.psum(array, axis)]
    all_to_all x0 -> x1, blocking collectives: none -> 10.1 us  [spread(): lax.all_to_all(jnp.stack([own] * lax.axis_size(axis)), axis, 0, 0)]
    all_to_all x0 -> x3, waiting for transfers between devices: none -> 6.95 us  [spread(): lax.all_to_all(jnp.stack([own] * lax.axis_size(axis)), axis, 0, 0)]
    all_gather x2 -> x0, waiting for transfers between devices: 5.51 us -> none  [spread(): lax.all_gather(own, axis, axis=0, tiled=True)[:len(lines)]]
    another operation x0 -> x4, local copies, waits for them, and re-layouts: none -> 5.48 us  [spread(): jnp.stack([own] * lax.axis_size(axis))]
  transfers between devices with their start and end apart: 8 -> 9, of which waited for: 5 -> 5; matrix products, arithmetic and copies ran while one was open for 6% -> 7% of each run, Pallas kernels for 0% -> 0%
where the time goes in v1:
time: 351 us; the launch traced here: 350 us
  waiting for transfers between devices  140 us (40%)
  blocking collectives  118 us (34%)
  starting transfers between devices  41.7 us (12%)
  local copies, waits for them, and re-layouts  22.1 us (6%)
  between operations  15.6 us (4%)
  matrix products  7.71 us (2%)
  other arithmetic  4.49 us (1%)
    psum x2, waiting for transfers between devices, broadcast_by_axis(): array = lax.psum(array, axis)  93 us
    psum x2, blocking collectives, broadcast_by_axis(): array = lax.psum(array, axis)  39.1 us
    all_to_all x1, waiting for transfers between devices, on_device(): lax.all_to_all(density_tiles, 'col', split_axis=1, concat_axis=0, tiled=T...  33.3 us
    unnamed x1, blocking collectives  24.2 us
    all_to_all x1, blocking collectives, sent_and_summed(): lax.all_to_all(pieces, axis, split_axis=0, concat_axis=0, tiled=True)  23.4 us
    all_to_all x3, starting transfers between devices, spread(): lax.all_to_all(jnp.stack([own] * lax.axis_size(axis)), axis, 0, 0)  21.5 us
    all_to_all x1, blocking collectives, on_device(): lax.all_to_all(summed.astype(jnp.bfloat16)[:, None], 'col', split_axis=0,...  21.2 us
    all_to_all x1, starting transfers between devices, on_device(): lax.all_to_all(tile_columns, 'col', split_axis=1, concat_axis=0, tiled=True)  10.2 us
  transfers between devices with their start and end apart: 9, of which 5 were waited for; matrix products, arithmetic and copies ran while one was open for 7% of the time, Pallas kernels for 0%

profile of v1, /device:TPU:1, one launch (start us, length us, event | category | flops | bytes accessed | tf_op | source)
XLA Modules:
  0.0 350.0 jit_solution(2816164539885409346)
XLA Ops:
  7.4 2.7 copy.171
  10.1 10.0 %all-to-all-start.2 = ((bf16[3,8,2,128,128]{4,3,2,0,1:T(8,128)(2,1)}), bf16[3,8,2,128,128]{4,3,2,0,1:T(8,128)(2,1)S(1)}, u32[]{:S(2)}, u32[]{:S(2)}) async-start(bf16[3,8,2,128,128]{4,3,2,0,1:T(8,128)(2,1)} %copy.171), calls=%async_computation.2 | async-start | bytes 3145728 | tf_op jit(solution)/shard_map/all_to_all | solution.py:66
  20.1 33.3 %all-to-all-done.2 = bf16[3,8,2,128,128]{4,3,2,0,1:T(8,128)(2,1)S(1)} async-done(((bf16[3,8,2,128,128]{4,3,2,0,1:T(8,128)(2,1)}), bf16[3,8,2,128,128]{4,3,2,0,1:T(8,128)(2,1)S(1)}, u32[]{:S(2)}, u32[]{:S(2)}) %all-to-all-start.2) | async-done | bytes 1572896 | tf_op jit(solution)/shard_map/all_to_all | solution.py:66
  53.4 2.8 broadcast_select_fusion.2
  58.3 10.2 %all-to-all-start = ((s32[3,8,2]{0,2,1:T(2,128)}), s32[3,8,2]{0,2,1:T(2,128)S(1)}, u32[]{:S(2)}, u32[]{:S(2)}) async-start(s32[3,8,2]{0,2,1:T(2,128)} %copy.157), calls=%async_computation | async-start | bytes 16384 | tf_op jit(solution)/shard_map/all_to_all | solution.py:67
  69.6 5.9 %all-to-all-done = s32[3,8,2]{0,2,1:T(2,128)S(1)} async-done(((s32[3,8,2]{0,2,1:T(2,128)}), s32[3,8,2]{0,2,1:T(2,128)S(1)}, u32[]{:S(2)}, u32[]{:S(2)}) %all-to-all-start) | async-done | bytes 224 | tf_op jit(solution)/shard_map/all_to_all | solution.py:67
  75.7 24.2 %all-reduce.2 = (s32[24,2]{1,0:T(8,128)S(1)}, s32[24,2]{1,0:T(8,128)S(1)}) all-reduce(s32[24,2]{1,0:T(8,128)S(1)} %get-tuple-element.34, s32[24,2]{1,0:T(8,128)S(1)} %get-tuple-element.36), channel_id=4, replica_groups=mesh['row_0'=4,'row_1'=2,'col'=8,'layer'=4] {'col'}, use_global_device_ids=true, to_apply=%region_10.11.clone | all-reduce | flops 96 | bytes 768
  100.6 8.8 %all-to-all-start.1 = ((s32[8,3,2]{1,2,0:T(2,128)}), s32[8,3,2]{1,2,0:T(2,128)S(1)}, u32[]{:S(2)}, u32[]{:S(2)}) async-start(s32[8,3,2]{1,2,0:T(2,128)} %stack.8), calls=%async_computation.1 | async-start | bytes 16384 | tf_op jit(solution)/shard_map/all_to_all | solution.py:23
  109.5 6.9 %all-to-all-done.1 = s32[8,3,2]{1,2,0:T(2,128)S(1)} async-done(((s32[8,3,2]{1,2,0:T(2,128)}), s32[8,3,2]{1,2,0:T(2,128)S(1)}, u32[]{:S(2)}, u32[]{:S(2)}) %all-to-all-start.1) | async-done | bytes 224 | tf_op jit(solution)/shard_map/all_to_all | solution.py:23
  116.5 10.1 %all_to_all.67 = s32[8,3,2]{1,2,0:T(2,128)S(1)} all-to-all(s32[8,3,2]{1,2,0:T(2,128)S(1)} %stack.10), channel_id=1, replica_groups=mesh['row_0'=4,'row_1'=2,'col'=8,'layer'=4] {'col'}, dimensions={0} | all-to-all | bytes 384 | tf_op jit(solution)/shard_map/all_to_all | solution.py:23
  126.6 2.4 stack.11
  128.9 4.2 %all-to-all-start.5 = ((bf16[8,768,128]{2,1,0:T(8,128)(2,1)}), bf16[8,768,128]{2,1,0:T(8,128)(2,1)S(1)}, u32[]{:S(2)}, u32[]{:S(2)}) async-start(bf16[8,768,128]{2,1,0:T(8,128)(2,1)} %stack.11), calls=%async_computation.7 | async-start | bytes 3145728 | tf_op jit(solution)/shard_map/all_to_all | solution.py:23
  133.1 9.7 %all-reduce.10.cloned.1.call-done = (bf16[24,2,128,128]{3,2,1,0:T(8,128)(2,1)}, bf16[24,2,128,128]{3,2,1,0:T(8,128)(2,1)}) async-done(((bf16[24,2,128,128]{3,2,1,0:T(8,128)(2,1)}, bf16[24,2,128,128]{3,2,1,0:T(8,128)(2,1)}), (bf16[24,2,128,128]{3,2,1,0:T(8,128)(2,1)}, bf16[24,2,128,128]{3,2,1,0:T(8,128)(2,1)})) %all-reduce.10.cloned.1.call-update) | async-done | bytes 3145744 | tf_op jit(solution)/shard_map/psum | solution.py:30
  143.0 12.7 %all-reduce.3 = (s32[24,2]{1,0:T(8,128)S(1)}, s32[24,2]{1,0:T(8,128)S(1)}) all-reduce(s32[24,2]{1,0:T(8,128)S(1)} %get-tuple-element.35, s32[24,2]{1,0:T(8,128)S(1)} %get-tuple-element.33), channel_id=1, replica_groups=mesh['row_0'=4,'row_1'=2,'col'=8,'layer'=4] {'row_0'}, use_global_device_ids=true, to_apply=%region_8.9 | all-reduce | flops 96 | bytes 768 | tf_op jit(solution)/shard_map/psum | solution.py:30
  155.7 26.4 %all-reduce.4 = (s32[24,2]{1,0:T(8,128)S(1)}, s32[24,2]{1,0:T(8,128)S(1)}) all-reduce(s32[24,2]{1,0:T(8,128)S(1)} %get-tuple-element.11, s32[24,2]{1,0:T(8,128)S(1)} %get-tuple-element.12), channel_id=1, replica_groups=mesh['row_0'=4,'row_1'=2,'col'=8,'layer'=4] {'row_1'}, use_global_device_ids=true, to_apply=%region_9.10 | all-reduce | flops 96 | bytes 768 | tf_op jit(solution)/shard_map/psum | solution.py:30
  182.2 2.5 stack.9
  184.7 8.5 %all-to-all-start.3 = ((bf16[8,768,128]{2,1,0:T(8,128)(2,1)}), bf16[8,768,128]{2,1,0:T(8,128)(2,1)}, u32[]{:S(2)}, u32[]{:S(2)}) async-start(bf16[8,768,128]{2,1,0:T(8,128)(2,1)} %stack.9), calls=%async_computation.4 | async-start | bytes 3145728 | tf_op jit(solution)/shard_map/all_to_all | solution.py:23
  198.0 83.3 %all-reduce.12.cloned.1.call-done = (bf16[24,2,128,128]{3,2,1,0:T(8,128)(2,1)}, bf16[24,2,128,128]{3,2,1,0:T(8,128)(2,1)}) async-done(((bf16[24,2,128,128]{3,2,1,0:T(8,128)(2,1)}, bf16[24,2,128,128]{3,2,1,0:T(8,128)(2,1)}), (bf16[24,2,128,128]{3,2,1,0:T(8,128)(2,1)}, bf16[24,2,128,128]{3,2,1,0:T(8,128)(2,1)})) %all-reduce.12.cloned.1.call-update) | async-done | bytes 3145744 | tf_op jit(solution)/shard_map/psum | solution.py:30
  281.3 4.5 %gather_fusion.3 = bf16[96,128,128]{2,1,0:T(8,128)(2,1)} fusion(bf16[24,2,128,128]{3,2,1,0:T(8,128)(2,1)} %get-tuple-element.17, s32[96]{0:T(128)S(1)} %reshape.187), kind=kCustom, calls=%fused_computation.3 | custom fusion | bytes 6292224 | tf_op jit(solution)/shard_map/gather | solution.py:56
  285.8 2.9 gather_fusion.1
  288.7 4.7 %fusion.1 = f32[24,2,128,128,1]{2,3,1,4,0:T(8,128)} fusion(bf16[24,2,128,128,1]{3,2,4,1,0:T(8,128)(2,1)} %bitcast.104, bf16[24,2,2,128,128]{4,3,2,1,0:T(8,128)(2,1)} %bitcast.101, pred[24,2,2]{2,1,0:T(4,128)(4,1)S(1)} %copy.186), kind=kOutput, calls=%fused_computation.6 | convolution fusion | flops 404226048 | bytes 7864416 | tf_op jit(solution)/shard_map/iarc,iascd->isrd/dot_general | solution.py:58
  293.4 3.0 fusion
  296.9 23.4 %all_to_all.68 = bf16[4,24,2,32,128]{4,3,2,1,0:T(8,128)(2,1)S(1)} all-to-all(bf16[4,24,2,32,128]{4,3,2,1,0:T(8,128)(2,1)S(1)} %bitcast.103), channel_id=1, replica_groups=mesh['row_0'=4,'row_1'=2,'col'=8,'layer'=4] {'layer'}, dimensions={0} | all-to-all | bytes 3145728 | tf_op jit(solution)/shard_map/all_to_all | solution.py:41
  320.6 21.2 %all_to_all.69 = bf16[24,1,2,32,128]{4,3,2,1,0:T(8,128)(2,1)S(1)} all-to-all(bf16[24,1,2,32,128]{4,3,2,1,0:T(8,128)(2,1)S(1)} %bitcast.110), channel_id=1, replica_groups=mesh['row_0'=4,'row_1'=2,'col'=8,'layer'=4] {'col'}, dimensions={0} | all-to-all | bytes 786432 | tf_op jit(solution)/shard_map/all_to_all | solution.py:97
  (79 shorter events, 10.1 us)
Async XLA Ops:
  10.1 43.3 %all-to-all-start.2 = ((bf16[3,8,2,128,128]{4,3,2,0,1:T(8,128)(2,1)}), bf16[3,8,2,128,128]{4,3,2,0,1:T(8,128)(2,1)S(1)}, u32[]{:S(2)}, u32[]{:S(2)}) async-start(bf16[3,8,2,128,128]{4,3,2,0,1:T(8,128)(2,1)} %copy.171), calls=%async_computation.2 | async-start | bytes 3145728 | tf_op jit(solution)/shard_map/all_to_all | solution.py:66
  20.1 106.5 %reduce-scatter.5.cloned.1.call-start = ((), (), s32[]{:S(2)}) async-start(), calls=%async_computation.11 | async-start | bytes 1769472 | tf_op jit(solution)/shard_map/reduce_scatter | solution.py:21
  56.2 86.6 %all-reduce.10.cloned.1.call-start = ((), (), s32[]{:S(2)}) async-start(), calls=%async_computation.12 | async-start | bytes 6291456 | tf_op jit(solution)/shard_map/psum | solution.py:30
  56.8 0.8 copy-start.1
  56.8 11.7 %copy-start.2 = (u32[256]{0:T(256)S(1)}, u32[256]{0:T(256)}, u32[]{:S(2)}) copy-start(u32[256]{0:T(256)} %constant.100) | copy-start | bytes 3076
  56.8 125.3 %reduce-scatter.3.cloned.1.call-start = ((), (), s32[]{:S(2)}) async-start(), calls=%async_computation.10 | async-start | bytes 1769472 | tf_op jit(solution)/shard_map/reduce_scatter | solution.py:21
  58.3 17.3 %all-to-all-start = ((s32[3,8,2]{0,2,1:T(2,128)}), s32[3,8,2]{0,2,1:T(2,128)S(1)}, u32[]{:S(2)}, u32[]{:S(2)}) async-start(s32[3,8,2]{0,2,1:T(2,128)} %copy.157), calls=%async_computation | async-start | bytes 16384 | tf_op jit(solution)/shard_map/all_to_all | solution.py:67
  100.6 15.8 %all-to-all-start.1 = ((s32[8,3,2]{1,2,0:T(2,128)}), s32[8,3,2]{1,2,0:T(2,128)S(1)}, u32[]{:S(2)}, u32[]{:S(2)}) async-start(s32[8,3,2]{1,2,0:T(2,128)} %stack.8), calls=%async_computation.1 | async-start | bytes 16384 | tf_op jit(solution)/shard_map/all_to_all | solution.py:23
  128.9 53.2 %all-to-all-start.5 = ((bf16[8,768,128]{2,1,0:T(8,128)(2,1)}), bf16[8,768,128]{2,1,0:T(8,128)(2,1)S(1)}, u32[]{:S(2)}, u32[]{:S(2)}) async-start(bf16[8,768,128]{2,1,0:T(8,128)(2,1)} %stack.11), calls=%async_computation.7 | async-start | bytes 3145728 | tf_op jit(solution)/shard_map/all_to_all | solution.py:23
  133.1 148.2 %all-reduce.12.cloned.1.call-start = ((), (), s32[]{:S(2)}) async-start(), calls=%async_computation.13 | async-start | bytes 6291456 | tf_op jit(solution)/shard_map/psum | solution.py:30
  182.2 2.5 copy-start
  184.7 108.7 %all-to-all-start.3 = ((bf16[8,768,128]{2,1,0:T(8,128)(2,1)}), bf16[8,768,128]{2,1,0:T(8,128)(2,1)}, u32[]{:S(2)}, u32[]{:S(2)}) async-start(bf16[8,768,128]{2,1,0:T(8,128)(2,1)} %stack.9), calls=%async_computation.4 | async-start | bytes 3145728 | tf_op jit(solution)/shard_map/all_to_all | solution.py:23
Sparse Core Ops, SparseCore 0:
  56.3 44.0 reduce-scatter.4
  103.0 42.9 reduce-scatter.2
Sparse Core Ops, SparseCore 1:
  59.1 83.7 all-reduce.9
  145.3 135.9 all-reduce.11
